TPU v7x, 32 devices: a whole 2x2x4 slice. The times are simulated.
32 devices in a mesh: dp: 16 (over z, y, x), tensor: 2 (over core).
Axes of the slice: x: 2, y: 2, z: 4, core: 2. Of those that a mesh axis runs over, the one named last changes fastest.
Arguments:
- residual: bfloat16 [512, 6144], P('dp', 'tensor'), may hold values from -16 to 16
- queries: bfloat16 [512, 6144], P('dp', 'tensor'), may hold values from -4.5 to 4.5
- keys: bfloat16 [512, 128, 1024], P('dp', None, 'tensor'), may hold values from -4.5 to 4.5
- values: bfloat16 [512, 128, 1024], P('dp', None, 'tensor'), may hold values from -6 to 6
- lengths: int32 [512], P('dp'), may hold values from 2 to 128
- norm_gain: bfloat16 [6144], P('tensor'), may hold values from 0.099609375 to 1.8984375
- expert_ids: int32 [512, 2], P('dp'), may hold values from 0 to 7, all different within a row; in each aligned block of 32 rows (0 to 31, 32 to 63, ...) at most 16 rows name the same one
- expert_weights: float32 [512, 2], P('dp'), may hold values from 0.2 to 1
- w_in: bfloat16 [6144, 65536], P('tensor', 'dp'), may hold values from -0.078125 to 0.078125
- w_out: bfloat16 [65536, 6144], P('dp', 'tensor'), may hold values from -0.0625 to 0.0625
Outputs:
- output: bfloat16 [512, 6144], P('dp', 'tensor')
Inputs may be any that keep to these rules, and one draw needn't show every extreme that they name: `expert_ids`: each token names 2 different experts; at most 16 of the tokens of one index of dp name one expert, and in every draw some expert is named by exactly 16 of them.
All inputs are finite; a program needn't handle non-finite values.
Results may differ from a plain program's by a relative error of at most 0.008.
Values may be sent and summed in bfloat16 or wider, within the bound.
A program may use at most 128 MiB of HBM per device.

v0:
```python
import jax
import jax.numpy as jnp
from jax import lax
from jax.sharding import PartitionSpec as P

D = 6144
HEADS = 48
KV = 8
HEAD = 128
EXPERTS = 8
TOPK = 2
CACHE = 128
SRC_CAP = 16


NORM_EPSILON = 1e-05


def prefix(part, axis, combine, identity):
    place = lax.axis_index(axis)
    gathered = lax.all_gather(part, axis)
    state = jnp.zeros_like(part) + jnp.asarray(identity, part.dtype)

    def one(lap, state):
        return combine(state, lax.dynamic_index_in_dim(gathered, lap, 0, False))

    return lax.fori_loop(0, place, one, state)


def add_counts(earlier, later):
    return earlier + later


def expert_rows(tok_rows, w_in, w_out):
    partial_sum = jnp.einsum("df,rd->fr", w_in, tok_rows, preferred_element_type=jnp.float32)
    hidden_total = lax.psum(partial_sum.astype(jnp.bfloat16), "tensor").astype(jnp.float32)
    hidden = jax.nn.silu(hidden_total).astype(jnp.bfloat16)
    return jnp.einsum("fr,fd->rd", hidden, w_out, preferred_element_type=jnp.float32)


def shards(
    residual, queries, keys, values, lengths, norm_gain, expert_ids, expert_weights, w_in, w_out
):
    tokens = residual.shape[0]
    width_local = residual.shape[1]
    head_groups = keys.shape[2] // HEAD
    group_size = HEADS // KV
    query_rows = queries.reshape(tokens, head_groups, group_size, HEAD)
    key_rows = keys.reshape(tokens, CACHE, head_groups, HEAD)
    value_rows = values.reshape(tokens, CACHE, head_groups, HEAD)
    scores = jnp.einsum(
        "tgjd,tlgd->tgjl", query_rows, key_rows, preferred_element_type=jnp.float32
    ) * HEAD ** (-0.5)
    live_mask = (jnp.arange(CACHE, dtype=jnp.int32)[None, :] < lengths[:, None])[:, None, None, :]
    scores = jnp.where(live_mask, scores, -1e30)
    peak_score = jnp.max(scores, axis=-1, keepdims=True)
    powered = jnp.exp(scores - peak_score)
    attention_probs = (powered / jnp.sum(powered, axis=-1, keepdims=True)).astype(jnp.bfloat16)
    attended = jnp.einsum(
        "tgjl,tlgd->tgjd", attention_probs, value_rows, preferred_element_type=jnp.float32
    )
    summed = residual.astype(jnp.float32) + attended.reshape(tokens, width_local)
    square_sums = lax.psum(jnp.sum(summed * summed, axis=1), "tensor")
    normed = (
        summed
        * lax.rsqrt(square_sums[:, None] / D + NORM_EPSILON)
        * norm_gain.astype(jnp.float32)[None, :]
    ).astype(jnp.bfloat16)
    flat_ids = expert_ids.reshape(-1)
    expert_iota = jnp.arange(EXPERTS, dtype=jnp.int32)
    onehot = (flat_ids[:, None] == expert_iota[None, :]).astype(jnp.int32)
    local_rank = jnp.sum(
        (jnp.cumsum(onehot, axis=0, dtype=jnp.int32) - onehot) * onehot, axis=1, dtype=jnp.int32
    )
    counts = jnp.sum(onehot, axis=0, dtype=jnp.int32)
    offsets = prefix(counts, "dp", add_counts, jnp.zeros_like(counts))
    slot_index = local_rank + jnp.sum(onehot * offsets[None, :], axis=1, dtype=jnp.int32)
    capacity = tokens * lax.axis_size("dp") * TOPK * 3 // (4 * EXPERTS)
    keep_mask = slot_index < capacity
    owners = lax.axis_size("dp") // EXPERTS
    slot_total = EXPERTS * SRC_CAP
    pair_target = flat_ids * SRC_CAP + local_rank
    pick_pairs = pair_target[None, :] == jnp.arange(slot_total, dtype=jnp.int32)[:, None]
    pick_tokens = jnp.sum(
        pick_pairs.reshape(slot_total, tokens, TOPK).astype(jnp.float32), axis=2
    ).astype(jnp.bfloat16)
    packed = jnp.dot(pick_tokens, normed, preferred_element_type=jnp.float32).astype(jnp.bfloat16)
    outgoing = jnp.broadcast_to(
        packed.reshape(EXPERTS, 1, SRC_CAP, width_local), (EXPERTS, owners, SRC_CAP, width_local)
    )
    outgoing = outgoing.reshape(EXPERTS * owners, SRC_CAP, width_local)
    received = lax.all_to_all(outgoing, "dp", split_axis=0, concat_axis=0, tiled=True)
    total_rows = received.shape[0] * received.shape[1]
    results = expert_rows(received.reshape(total_rows, width_local), w_in, w_out)
    returned = results.reshape(received.shape[0], SRC_CAP, width_local)
    combined = lax.all_to_all(
        returned.astype(jnp.bfloat16), "dp", split_axis=0, concat_axis=0, tiled=True
    ).astype(returned.dtype)
    per_expert = jnp.sum(combined.reshape(EXPERTS, owners, SRC_CAP, width_local), axis=1).reshape(
        slot_total, width_local
    )
    pair_weight = expert_weights.reshape(-1) * keep_mask.astype(jnp.float32)
    mix_rows = jnp.sum(
        (pick_pairs.astype(jnp.float32) * pair_weight[None, :]).reshape(slot_total, tokens, TOPK),
        axis=2,
    )
    addition = jnp.einsum("st,sd->td", mix_rows, per_expert, precision=lax.Precision.HIGHEST)
    return (summed + addition).astype(jnp.bfloat16)


def solution(mesh):
    in_specs = (
        P("dp", "tensor"),
        P("dp", "tensor"),
        P("dp", None, "tensor"),
        P("dp", None, "tensor"),
        P("dp"),
        P("tensor"),
        P("dp", None),
        P("dp", None),
        P("tensor", "dp"),
        P("dp", "tensor"),
    )
    out_specs = P("dp", "tensor")
    return jax.shard_map(shards, mesh=mesh, in_specs=in_specs, out_specs=out_specs, check_vma=False)
```

profile of v0, /device:TPU:0, one launch (start us, length us, event | category | flops | bytes accessed | tf_op | source)
XLA Modules:
  0.0 180.8 jit_solution(6086627197087808506)
XLA Ops:
  6.5 0.8 copy.37
  7.3 0.1 eq.30
  7.6 0.7 iota_compare_fusion.2
  8.3 0.7 convert_element_type.53
  9.0 1.2 dynamic-slice
  10.8 0.2 dynamic-update-slice
  11.1 16.2 %all-reduce = s32[128]{0:T(128)S(1)} all-reduce(s32[128]{0:T(128)S(1)} %dynamic-update-slice), channel_id=2, replica_groups=mesh['dp'=16,'tensor'=2] {'dp'}, use_global_device_ids=true, to_apply=%add | all-reduce | flops 128 | bytes 1024
  27.5 0.2 select_reduce_fusion.1
  27.8 0.1 reduce_sum.78
  28.0 0.7 multiply_add_fusion
  28.7 1.2 reshape.102
  29.9 4.6 %fusion.30 = (f32[32,4,6]{2,1,0:T(4,128)S(1)}, f32[32,4,6,128]{3,2,1,0:T(8,128)S(1)}) fusion(bf16[32,4,6,128]{3,2,1,0:T(8,128)(2,1)S(1)} %reshape.102, pred[32,128]{1,0:T(8,128)(4,1)S(1)} %iota_compare_fusion.2, bf16[32,128,512]{2,1,0:T(8,128)(2,1)} %param.14), kind=kOutput, calls=%fused_computation.47 | convolution fusion | flops 25559168 | bytes 4791296 | tf_op jit(solution)/shard_map/sub | solution.py:57
  34.6 3.5 %fusion.6 = f32[32,4,6,128]{3,2,1,0:T(8,128)S(1)} fusion(f32[32,4,6,128]{3,2,1,0:T(8,128)S(1)} %get-tuple-element.42, f32[32,4,6]{2,1,0:T(4,128)S(1)} %get-tuple-element.41, bf16[32,128,512]{2,1,0:T(8,128)(2,1)} %param.15), kind=kOutput, calls=%fused_computation.10 | convolution fusion | flops 25362432 | bytes 4983808 | tf_op jit(solution)/shard_map/tgjl,tlgd->tgjd/dot_general | solution.py:59
  38.2 0.2 multiply_reduce_fusion
  38.3 2.5 %psum.14 = f32[32]{0:T(128)S(1)} all-reduce(f32[32]{0:T(128)S(1)} %multiply_reduce_fusion), channel_id=1, replica_groups=mesh['dp'=16,'tensor'=2] {'tensor'}, use_global_device_ids=true, to_apply=%region_11.12 | all-reduce | flops 32 | bytes 256 | tf_op jit(solution)/shard_map/psum | solution.py:63
  40.9 0.4 convolution_convert_fusion.2
  41.3 0.2 broadcast_in_dim.19
  41.5 40.8 %all_to_all.10 = bf16[16,16,3072]{2,1,0:T(8,128)(2,1)S(1)} all-to-all(bf16[16,16,3072]{2,1,0:T(8,128)(2,1)S(1)} %bitcast.44), channel_id=1, replica_groups=mesh['dp'=16,'tensor'=2] {'dp'}, dimensions={0} | all-to-all | bytes 3145728 | tf_op jit(solution)/shard_map/all_to_all | solution.py:92
  82.3 13.2 %fusion.1 = bf16[4096,256]{0,1:T(8,128)(2,1)} fusion(bf16[256,3072]{1,0:T(8,128)(2,1)S(1)} %bitcast.46, bf16[3072,4096]{1,0:T(8,128)(2,1)} %param.20), kind=kOutput, calls=%fused_computation.5 | convolution fusion | flops 6443499520 | bytes 28835840 | tf_op jit(solution)/shard_map/df,rd->fr/dot_general | solution.py:35
  95.5 19.7 %all-reduce.3.cloned.1.call-done = bf16[4096,256]{0,1:T(8,128)(2,1)} async-done(((bf16[4096,256]{0,1:T(8,128)(2,1)}), bf16[4096,256]{0,1:T(8,128)(2,1)}) %all-reduce.3.cloned.1.call-update) | async-done | bytes 2097168 | tf_op jit(solution)/shard_map/psum | solution.py:36
  115.3 12.2 %convolution_convert_fusion.1 = bf16[256,3072]{1,0:T(8,128)(2,1)S(1)} fusion(bf16[4096,3072]{1,0:T(8,128)(2,1)} %param.21, bf16[4096,256]{0,1:T(8,128)(2,1)} %all-reduce.3.cloned.1.call-done), kind=kOutput, calls=%fused_computation.16 | convolution fusion | flops 6449528832 | bytes 28835840 | tf_op jit(solution)/shard_map/fr,fd->rd/dot_general | solution.py:38
  127.5 44.6 %all_to_all.11 = bf16[16,16,3072]{2,1,0:T(8,128)(2,1)S(1)} all-to-all(bf16[16,16,3072]{2,1,0:T(8,128)(2,1)S(1)} %bitcast.47), channel_id=1, replica_groups=mesh['dp'=16,'tensor'=2] {'dp'}, dimensions={0} | all-to-all | bytes 3145728 | tf_op jit(solution)/shard_map/all_to_all | solution.py:96
  172.0 0.3 convert_reduce_fusion
  172.4 1.6 fusion.12
  (20 shorter events, 0.8 us)
Async XLA Ops:
  6.5 108.7 %all-reduce.3.cloned.1.call-start = ((), (), s32[]{:S(2)}) async-start(), calls=%async_computation.2 | async-start | bytes 4194304 | tf_op jit(solution)/shard_map/psum | solution.py:36
  34.5 3.6 %copy-start = (bf16[32,3072]{1,0:T(8,128)(2,1)S(1)}, bf16[32,3072]{1,0:T(8,128)(2,1)}, u32[]{:S(2)}) copy-start(bf16[32,3072]{1,0:T(8,128)(2,1)} %param.12) | copy-start | bytes 589828
  34.6 6.2 %copy-start.1 = (f32[32,2]{0,1:T(2,128)S(1)}, f32[32,2]{0,1:T(2,128)}, u32[]{:S(2)}) copy-start(f32[32,2]{0,1:T(2,128)} %param.19) | copy-start | bytes 772
Sparse Core Ops, SparseCore 0:
  95.6 19.5 all-reduce.2
where the time goes:
time: 181 us
  blocking collectives  104 us (57%)
  matrix products  35.5 us (20%)
  waiting for transfers between devices  19.8 us (11%)
  between operations  14.1 us (8%)
  local copies, waits for them, and re-layouts  4.26 us (2%)
  other arithmetic  3.15 us (2%)
    all_to_all x1, blocking collectives, shards(): lax.all_to_all(returned.astype(jnp.bfloat16), 'dp', split_axis=0, concat_...  44.6 us
    all_to_all x1, blocking collectives, shards(): lax.all_to_all(outgoing, 'dp', split_axis=0, concat_axis=0, tiled=True)  40.8 us
    psum x1, waiting for transfers between devices, expert_rows(): lax.psum(partial_sum.astype(jnp.bfloat16), 'tensor').astype(jnp.float32)  19.7 us
    unnamed x1, blocking collectives  16.2 us
    dot_general x1, matrix products, expert_rows(): jnp.einsum('df,rd->fr', w_in, tok_rows, preferred_element_type=jnp.float32)  13.2 us
    dot_general x1, matrix products, expert_rows(): jnp.einsum('fr,fd->rd', hidden, w_out, preferred_element_type=jnp.float32)  12.2 us
    sub x1, matrix products, shards(): powered = jnp.exp(scores - peak_score)  4.65 us
  transfers between devices with their start and end apart: 1, of which 1 were waited for; matrix products, arithmetic and copies ran while one was open for 0% of the time, Pallas kernels for 0%

commit v1 on v0

--- a/solution.py
+++ b/solution.py
@@ -1,6 +1,10 @@
+import functools
+
 import jax
 import jax.numpy as jnp
 from jax import lax
+from jax.experimental import pallas as pl
+from jax.experimental.pallas import tpu as pltpu
 from jax.sharding import PartitionSpec as P
 
 D = 6144
@@ -16,26 +20,187 @@
 NORM_EPSILON = 1e-05
 
 
-def prefix(part, axis, combine, identity):
-    place = lax.axis_index(axis)
-    gathered = lax.all_gather(part, axis)
-    state = jnp.zeros_like(part) + jnp.asarray(identity, part.dtype)
-
-    def one(lap, state):
-        return combine(state, lax.dynamic_index_in_dim(gathered, lap, 0, False))
-
-    return lax.fori_loop(0, place, one, state)
-
-
-def add_counts(earlier, later):
-    return earlier + later
+MESH = pl.DeviceIdType.MESH
+
+
+def remote(source, target, send_sem, recv_sem, place):
+    return pltpu.make_async_remote_copy(
+        src_ref=source,
+        dst_ref=target,
+        send_sem=send_sem,
+        recv_sem=recv_sem,
+        device_id={"dp": place},
+        device_id_type=MESH,
+    )
+
+
+def greet(places):
+    barrier = pltpu.get_barrier_semaphore()
+    for place in places:
+        pl.semaphore_signal(barrier, inc=1, device_id={"dp": place}, device_id_type=MESH)
+    pl.semaphore_wait(barrier, len(places))
+
+
+def far_first(amount):
+    return sorted(range(1, amount), key=lambda lap: (-min(lap, amount - lap), lap))
+
+
+def dispatch_kernel(owners, packed, counts, received, all_counts, plane_send, plane_recv,
+                    pair_send, pair_recv, count_send, count_recv, own_sem):
+    experts = packed.shape[0]
+    places = experts * owners
+    me = lax.axis_index("dp")
+    expert, owner = lax.div(me, owners), lax.rem(me, owners)
+    greet([lax.rem(me + lap, places) for lap in range(1, places)])
+    waiting = []
+    for lap in range(1, places):
+        copy = remote(counts, all_counts.at[me], count_send.at[lap], count_recv.at[lap],
+                      lax.rem(me + lap, places))
+        copy.start()
+        waiting.append(copy)
+    own = pltpu.make_async_copy(packed.at[expert], received.at[me], own_sem)
+    own.start()
+    own_count = pltpu.make_async_copy(counts, all_counts.at[me], count_recv.at[0])
+    own_count.start()
+
+    def forward(source, place, lap):
+        for step in range(1, owners):
+            other = lax.rem(owner + step, owners)
+            spot = lap * owners + step
+            copy = remote(source, received.at[place], pair_send.at[spot], pair_recv.at[spot],
+                          expert * owners + other)
+            copy.start()
+            waiting.append(copy)
+
+    forward(packed.at[expert], me, 0)
+    middle = far_first(experts)
+    order = [lap for lap in middle if lap in (1, experts - 1)]
+    order += [lap for lap in middle if lap not in (1, experts - 1)]
+    for lap in order:
+        target = lax.rem(expert + lap, experts)
+        copy = remote(packed.at[target], received.at[me], plane_send.at[lap], plane_recv.at[lap],
+                      target * owners + owner)
+        copy.start()
+        waiting.append(copy)
+    for lap in order:
+        source = lax.rem(expert + experts - lap, experts) * owners + owner
+        remote(received.at[source], received.at[source], plane_send.at[lap], plane_recv.at[lap],
+               source).wait_recv()
+        forward(received.at[source], source, lap)
+    for lap in [0] + order:
+        for step in range(1, owners):
+            other = lax.rem(owner + owners - step, owners)
+            place = lax.rem(expert + experts - lap, experts) * owners + other
+            spot = lap * owners + step
+            remote(received.at[place], received.at[place], pair_send.at[spot], pair_recv.at[spot],
+                   expert * owners + other).wait_recv()
+    for lap in range(1, places):
+        source = lax.rem(me + places - lap, places)
+        remote(counts, all_counts.at[source], count_send.at[lap], count_recv.at[lap],
+               source).wait_recv()
+    own.wait()
+    own_count.wait()
+    for copy in waiting:
+        copy.wait_send()
+
+
+def dispatch(packed, counts, owners):
+    experts, rows, width = packed.shape
+    places = experts * owners
+    dma = pltpu.SemaphoreType.DMA
+    vmem = pl.BlockSpec(memory_space=pltpu.VMEM)
+    return pl.pallas_call(
+        functools.partial(dispatch_kernel, owners),
+        out_shape=(
+            jax.ShapeDtypeStruct((places, rows, width), packed.dtype),
+            jax.ShapeDtypeStruct((places,) + counts.shape, counts.dtype),
+        ),
+        in_specs=[vmem, vmem],
+        out_specs=(vmem, vmem),
+        scratch_shapes=[
+            dma((experts,)),
+            dma((experts,)),
+            dma((places,)),
+            dma((places,)),
+            dma((places,)),
+            dma((places,)),
+            dma,
+        ],
+        compiler_params=pltpu.CompilerParams(collective_id=0, has_side_effects=True),
+    )(packed, counts)
+
+
+def return_kernel(owners, part, out, landed, total, pair_send, pair_recv, plane_send, plane_recv):
+    experts = out.shape[0]
+    me = lax.axis_index("dp")
+    expert, owner = lax.div(me, owners), lax.rem(me, owners)
+    greet(
+        [lax.rem(expert + lap, experts) * owners + owner for lap in range(1, experts)]
+        + [expert * owners + lax.rem(owner + step, owners) for step in range(1, owners)]
+    )
+    order = far_first(experts) + [0]
+    waiting = []
+    for lap in order:
+        for step in range(1, owners):
+            other = lax.rem(owner + step, owners)
+            source = lax.rem(expert + lap, experts) * owners + other
+            spot = lap * owners + step
+            copy = remote(part.at[source], landed.at[spot], pair_send.at[spot], pair_recv.at[spot],
+                          expert * owners + other)
+            copy.start()
+            waiting.append(copy)
+    for lap in order:
+        target = lax.rem(expert + lap, experts) * owners + owner
+        value = part[target].astype(jnp.float32)
+        for step in range(1, owners):
+            other = lax.rem(owner + owners - step, owners)
+            spot = lap * owners + step
+            remote(landed.at[spot], landed.at[spot], pair_send.at[spot], pair_recv.at[spot],
+                   expert * owners + other).wait_recv()
+            value += landed[spot].astype(jnp.float32)
+        if lap == 0:
+            out[expert] = value.astype(out.dtype)
+        else:
+            total[lap] = value.astype(total.dtype)
+            copy = remote(total.at[lap], out.at[expert], plane_send.at[lap], plane_recv.at[lap],
+                          target)
+            copy.start()
+            waiting.append(copy)
+    for lap in order[:-1]:
+        source = lax.rem(expert + experts - lap, experts)
+        remote(total.at[lap], out.at[source], plane_send.at[lap], plane_recv.at[lap],
+               source * owners + owner).wait_recv()
+    for copy in waiting:
+        copy.wait_send()
+
+
+def send_back(part, owners):
+    places, rows, width = part.shape
+    experts = places // owners
+    dma = pltpu.SemaphoreType.DMA
+    vmem = pl.BlockSpec(memory_space=pltpu.VMEM)
+    return pl.pallas_call(
+        functools.partial(return_kernel, owners),
+        out_shape=jax.ShapeDtypeStruct((experts, rows, width), part.dtype),
+        in_specs=[vmem],
+        out_specs=vmem,
+        scratch_shapes=[
+            pltpu.VMEM((places, rows, width), part.dtype),
+            pltpu.VMEM((experts, rows, width), part.dtype),
+            dma((places,)),
+            dma((places,)),
+            dma((experts,)),
+            dma((experts,)),
+        ],
+        compiler_params=pltpu.CompilerParams(collective_id=1, has_side_effects=True),
+    )(part)
 
 
 def expert_rows(tok_rows, w_in, w_out):
-    partial_sum = jnp.einsum("df,rd->fr", w_in, tok_rows, preferred_element_type=jnp.float32)
+    partial_sum = jnp.einsum("rd,df->rf", tok_rows, w_in, preferred_element_type=jnp.float32)
     hidden_total = lax.psum(partial_sum.astype(jnp.bfloat16), "tensor").astype(jnp.float32)
     hidden = jax.nn.silu(hidden_total).astype(jnp.bfloat16)
-    return jnp.einsum("fr,fd->rd", hidden, w_out, preferred_element_type=jnp.float32)
+    return jnp.einsum("rf,fd->rd", hidden, w_out, preferred_element_type=jnp.float32)
 
 
 def shards(
@@ -73,11 +238,10 @@
         (jnp.cumsum(onehot, axis=0, dtype=jnp.int32) - onehot) * onehot, axis=1, dtype=jnp.int32
     )
     counts = jnp.sum(onehot, axis=0, dtype=jnp.int32)
-    offsets = prefix(counts, "dp", add_counts, jnp.zeros_like(counts))
-    slot_index = local_rank + jnp.sum(onehot * offsets[None, :], axis=1, dtype=jnp.int32)
-    capacity = tokens * lax.axis_size("dp") * TOPK * 3 // (4 * EXPERTS)
-    keep_mask = slot_index < capacity
-    owners = lax.axis_size("dp") // EXPERTS
+    places = lax.axis_size("dp")
+    me = lax.axis_index("dp")
+    owners = places // EXPERTS
+    capacity = tokens * places * TOPK * 3 // (4 * EXPERTS)
     slot_total = EXPERTS * SRC_CAP
     pair_target = flat_ids * SRC_CAP + local_rank
     pick_pairs = pair_target[None, :] == jnp.arange(slot_total, dtype=jnp.int32)[:, None]
@@ -85,19 +249,40 @@
         pick_pairs.reshape(slot_total, tokens, TOPK).astype(jnp.float32), axis=2
     ).astype(jnp.bfloat16)
     packed = jnp.dot(pick_tokens, normed, preferred_element_type=jnp.float32).astype(jnp.bfloat16)
-    outgoing = jnp.broadcast_to(
-        packed.reshape(EXPERTS, 1, SRC_CAP, width_local), (EXPERTS, owners, SRC_CAP, width_local)
-    )
-    outgoing = outgoing.reshape(EXPERTS * owners, SRC_CAP, width_local)
-    received = lax.all_to_all(outgoing, "dp", split_axis=0, concat_axis=0, tiled=True)
-    total_rows = received.shape[0] * received.shape[1]
-    results = expert_rows(received.reshape(total_rows, width_local), w_in, w_out)
-    returned = results.reshape(received.shape[0], SRC_CAP, width_local)
-    combined = lax.all_to_all(
-        returned.astype(jnp.bfloat16), "dp", split_axis=0, concat_axis=0, tiled=True
-    ).astype(returned.dtype)
-    per_expert = jnp.sum(combined.reshape(EXPERTS, owners, SRC_CAP, width_local), axis=1).reshape(
-        slot_total, width_local
+    padded_counts = jnp.pad(counts[None, :], ((0, 0), (0, 128 - EXPERTS)))
+    received, gathered = dispatch(
+        packed.reshape(EXPERTS, SRC_CAP, width_local), padded_counts, owners
+    )
+    all_counts = gathered[:, 0, :EXPERTS]
+    place_iota = jnp.arange(places, dtype=jnp.int32)
+    offsets = jnp.sum(jnp.where(place_iota[:, None] < me, all_counts, 0), axis=0, dtype=jnp.int32)
+    slot_index = local_rank + jnp.sum(onehot * offsets[None, :], axis=1, dtype=jnp.int32)
+    keep_mask = slot_index < capacity
+    mine = jnp.sum(
+        jnp.where(expert_iota[None, :] == me // owners, all_counts, 0), axis=1, dtype=jnp.int32
+    )
+    before = jnp.sum(
+        jnp.where(place_iota[None, :] < place_iota[:, None], mine[None, :], 0),
+        axis=1,
+        dtype=jnp.int32,
+    )
+    rank = jnp.arange(SRC_CAP, dtype=jnp.int32)[None, :]
+    row_slot = jnp.where(rank < mine[:, None], before[:, None] + rank, -1).reshape(-1)
+    pick_rows = (
+        row_slot[None, :] == jnp.arange(capacity, dtype=jnp.int32)[:, None]
+    ).astype(jnp.bfloat16)
+    total_rows = places * SRC_CAP
+    compact = jnp.dot(
+        pick_rows, received.reshape(total_rows, width_local), preferred_element_type=jnp.float32
+    ).astype(jnp.bfloat16)
+    results = expert_rows(compact, w_in, w_out).astype(jnp.bfloat16)
+    spread = jnp.einsum(
+        "cr,cd->rd", pick_rows, results, preferred_element_type=jnp.float32
+    ).astype(jnp.bfloat16)
+    per_expert = (
+        send_back(spread.reshape(places, SRC_CAP, width_local), owners)
+        .reshape(slot_total, width_local)
+        .astype(jnp.float32)
     )
     pair_weight = expert_weights.reshape(-1) * keep_mask.astype(jnp.float32)
     mix_rows = jnp.sum(

time: 181 us -> 143 us (0.79)
  blocking collectives: 104 us -> 2.62 us
  Pallas kernels: 0 us -> 64.2 us
  matrix products: 35.5 us -> 37.7 us
  waiting for transfers between devices: 19.8 us -> 17.7 us
    all_to_all x2 -> x0, blocking collectives: 85.3 us -> none  [the longest x1 44.6 us: shards(): lax.all_to_all(returned.astype(jnp.bfloat16), 'dp', split_axis=0, concat_...]
    pallas_call x0 -> x2, Pallas kernels: none -> 64.2 us  [the longest x1 35.4 us: dispatch(): pl.pallas_call(functools.partial(dispatch_kernel, owners), out_shape=(jax...]
    unnamed x1 -> x0, blocking collectives: 16.2 us -> none
    psum x1, waiting for transfers between devices: 19.7 us -> 17.7 us  [expert_rows(): lax.psum(partial_sum.astype(jnp.bfloat16), 'tensor').astype(jnp.float32)]
where the time goes in v1:
time: 143 us; the launch traced here: 142 us
  Pallas kernels  64.2 us (45%)
  matrix products  37.7 us (26%)
  waiting for transfers between devices  17.7 us (12%)
  between operations  13.5 us (9%)
  local copies, waits for them, and re-layouts  3.9 us (3%)
  other arithmetic  2.65 us (2%)
  blocking collectives  2.62 us (2%)
    pallas_call x1, Pallas kernels, dispatch(): pl.pallas_call(functools.partial(dispatch_kernel, owners), out_shape=(jax...  35.4 us
    pallas_call x1, Pallas kernels, send_back(): pl.pallas_call(functools.partial(return_kernel, owners), out_shape=jax.Sh...  28.8 us
    psum x1, waiting for transfers between devices, expert_rows(): lax.psum(partial_sum.astype(jnp.bfloat16), 'tensor').astype(jnp.float32)  17.7 us
    dot_general x1, matrix products, shards(): jnp.einsum('cr,cd->rd', pick_rows, results, preferred_element_type=jnp.fl...  14.1 us
    dot_general x1, matrix products, expert_rows(): jnp.einsum('rd,df->rf', tok_rows, w_in, preferred_element_type=jnp.float32)  11.9 us
    sub x1, matrix products, shards(): powered = jnp.exp(scores - peak_score)  4.64 us
    dot_general x1, matrix products, shards(): jnp.einsum('tgjl,tlgd->tgjd', attention_probs, value_rows, preferred_elem...  3.47 us
  transfers between devices with their start and end apart: 1, of which 1 were waited for; matrix products, arithmetic and copies ran while one was open for 0% of the time, Pallas kernels for 0%

profile of v1, /device:TPU:0, one launch (start us, length us, event | category | flops | bytes accessed | tf_op | source)
XLA Modules:
  0.0 142.3 jit_solution(14939147411546252572)
XLA Ops:
  6.5 0.8 copy.40
  7.3 0.1 eq.54
  7.6 0.2 fusion.31
  7.8 0.1 reduce_sum.96
  8.0 0.7 multiply_add_fusion
  8.7 1.2 reshape.139
  9.9 0.7 iota_compare_fusion.6
  10.7 4.6 %fusion.37 = (f32[32,4,6]{2,1,0:T(4,128)S(1)}, f32[32,4,6,128]{3,2,1,0:T(8,128)S(1)}) fusion(bf16[32,4,6,128]{3,2,1,0:T(8,128)(2,1)S(1)} %reshape.139, pred[32,128]{1,0:T(8,128)(4,1)S(1)} %iota_compare_fusion.6, bf16[32,128,512]{2,1,0:T(8,128)(2,1)} %param.12), kind=kOutput, calls=%fused_computation.59 | convolution fusion | flops 25559168 | bytes 4791296 | tf_op jit(solution)/shard_map/sub | solution.py:222
  15.3 3.5 %fusion.1 = f32[32,4,6,128]{3,2,1,0:T(8,128)S(1)} fusion(f32[32,4,6,128]{3,2,1,0:T(8,128)S(1)} %get-tuple-element.14, f32[32,4,6]{2,1,0:T(4,128)S(1)} %get-tuple-element.13, bf16[32,128,512]{2,1,0:T(8,128)(2,1)} %param.13), kind=kOutput, calls=%fused_computation.2 | convolution fusion | flops 25362432 | bytes 4983808 | tf_op jit(solution)/shard_map/tgjl,tlgd->tgjd/dot_general | solution.py:224
  18.9 0.2 multiply_reduce_fusion
  19.1 2.6 %psum.14 = f32[32]{0:T(128)S(1)} all-reduce(f32[32]{0:T(128)S(1)} %multiply_reduce_fusion), channel_id=1, replica_groups=mesh['dp'=16,'tensor'=2] {'tensor'}, use_global_device_ids=true, to_apply=%region_6.7 | all-reduce | flops 32 | bytes 256 | tf_op jit(solution)/shard_map/psum | solution.py:228
  21.7 0.5 pad.4.counts
  22.3 1.3 convolution_convert_fusion.2
  23.6 35.4 %shard_map.100 = (bf16[16,16,3072]{2,1,0:T(8,128)(2,1)}, s32[16,1,128]{2,1,0:T(1,128)}) custom-call(bf16[8,16,3072]{2,1,0:T(8,128)(2,1)} %bitcast.42, s32[1,128]{1,0:T(1,128)} %pad.4.counts), custom_call_target="tpu_custom_call" | custom-call | tf_op jit(solution)/shard_map/pallas_call | solution.py:112
  59.0 0.8 copy.42
  59.8 0.1 fusion.34
  59.9 0.1 select_reduce_fusion.3
  60.2 11.9 %convolution_convert_fusion = bf16[96,4096]{1,0:T(8,128)(2,1)} fusion(bf16[3072,4096]{1,0:T(8,128)(2,1)} %param.18, bf16[256,3072]{1,0:T(8,128)(2,1)} %bitcast.41, s32[256]{0:T(256)S(1)} %select_n.38), kind=kOutput, calls=%fused_computation.1 | convolution fusion | flops 2567626752 | bytes 27526144 | tf_op jit(solution)/shard_map/rd,df->rf/dot_general | solution.py:200
  72.1 0.2 select_reduce_fusion.1
  72.3 0.1 reduce_sum.102
  72.6 17.7 %all-reduce.3.cloned.1.call-done = bf16[96,4096]{1,0:T(8,128)(2,1)} async-done(((bf16[96,4096]{1,0:T(8,128)(2,1)}), bf16[96,4096]{1,0:T(8,128)(2,1)}) %all-reduce.3.cloned.1.call-update) | async-done | bytes 786448 | tf_op jit(solution)/shard_map/psum | solution.py:201
  90.3 14.1 %convolution_convert_fusion.1 = bf16[256,3072]{1,0:T(8,128)(2,1)} fusion(bf16[4096,3072]{1,0:T(8,128)(2,1)} %param.19, bf16[96,4096]{1,0:T(8,128)(2,1)} %all-reduce.3.cloned.1.call-done, s32[256]{0:T(256)S(1)} %select_n.38), kind=kOutput, calls=%fused_computation.8 | convolution fusion | flops 2570379264 | bytes 27526144 | tf_op jit(solution)/shard_map/cr,cd->rd/dot_general | solution.py:279
  104.4 28.8 %shard_map.101 = bf16[8,16,3072]{2,1,0:T(8,128)(2,1)} custom-call(bf16[16,16,3072]{2,1,0:T(8,128)(2,1)} %bitcast.44), custom_call_target="tpu_custom_call" | custom-call | tf_op jit(solution)/shard_map/pallas_call | solution.py:182
  133.2 2.2 %fusion.7 = bf16[32,3072]{1,0:T(8,128)(2,1)} fusion(f32[128,32]{0,1:T(8,128)S(1)} %select_reduce_fusion, bf16[128,3072]{1,0:T(8,128)(2,1)} %bitcast.43, f32[32,3072]{1,0:T(8,128)S(1)} %reshape.142, bf16[32,3072]{1,0:T(8,128)(2,1)S(1)} %copy-done), kind=kOutput, calls=%fused_computation.13 | convolution fusion | flops 151388160 | bytes 1589248 | tf_op jit(solution)/shard_map/st,sd->td/dot_general | solution.py:292
  (22 shorter events, 0.8 us)
Async XLA Ops:
  6.5 83.8 %all-reduce.3.cloned.1.call-start = ((), (), s32[]{:S(2)}) async-start(), calls=%async_computation | async-start | bytes 1572864 | tf_op jit(solution)/shard_map/psum | solution.py:201
  15.3 3.6 %copy-start = (bf16[32,3072]{1,0:T(8,128)(2,1)S(1)}, bf16[32,3072]{1,0:T(8,128)(2,1)}, u32[]{:S(2)}) copy-start(bf16[32,3072]{1,0:T(8,128)(2,1)} %param.10) | copy-start | bytes 589828
  15.3 6.4 %copy-start.1 = (bf16[3072]{0:T(1024)(128)(2,1)S(1)}, bf16[3072]{0:T(1024)(128)(2,1)}, u32[]{:S(2)}) copy-start(bf16[3072]{0:T(1024)(128)(2,1)} %param.15) | copy-start | bytes 18436
  60.2 12.3 %copy-start.2 = (f32[32,2]{0,1:T(2,128)S(1)}, f32[32,2]{0,1:T(2,128)}, u32[]{:S(2)}) copy-start(f32[32,2]{0,1:T(2,128)} %param.17) | copy-start | bytes 772
Sparse Core Ops, SparseCore 0:
  72.3 17.9 all-reduce.2

commit v2 on v1

--- a/solution.py
+++ b/solution.py
@@ -196,10 +196,72 @@
     )(part)
 
 
+def hidden_kernel(members, chunk, part, out, landed, send_sem, recv_sem):
+    me = lax.axis_index("tensor")
+    barrier = pltpu.get_barrier_semaphore()
+    for step in range(1, members):
+        pl.semaphore_signal(
+            barrier,
+            inc=1,
+            device_id={"tensor": lax.rem(me + step, members)},
+            device_id_type=MESH,
+        )
+    pl.semaphore_wait(barrier, members - 1)
+
+    def piece_copy(piece, step):
+        rows = pl.ds(piece * chunk, chunk)
+        spot = piece * members + step
+        return pltpu.make_async_remote_copy(
+            src_ref=part.at[rows],
+            dst_ref=landed.at[step, rows],
+            send_sem=send_sem.at[spot],
+            recv_sem=recv_sem.at[spot],
+            device_id={"tensor": lax.rem(me + step, members)},
+            device_id_type=MESH,
+        )
+
+    copies = [
+        [piece_copy(piece, step) for step in range(1, members)]
+        for piece in range(part.shape[0] // chunk)
+    ]
+    for row in copies:
+        for copy in row:
+            copy.start()
+    for piece, row in enumerate(copies):
+        rows = pl.ds(piece * chunk, chunk)
+        value = part[rows].astype(jnp.float32)
+        for step, copy in enumerate(row, 1):
+            copy.wait_recv()
+            value += landed[step, rows].astype(jnp.float32)
+        out[rows] = (value / (1.0 + jnp.exp(-value))).astype(out.dtype)
+    for row in copies:
+        for copy in row:
+            copy.wait_send()
+
+
+def hidden_rows(part):
+    members = lax.axis_size("tensor")
+    rows = part.shape[0]
+    chunk = 32 if rows % 32 == 0 else rows
+    dma = pltpu.SemaphoreType.DMA
+    vmem = pl.BlockSpec(memory_space=pltpu.VMEM)
+    return pl.pallas_call(
+        functools.partial(hidden_kernel, members, chunk),
+        out_shape=jax.ShapeDtypeStruct(part.shape, part.dtype),
+        in_specs=[vmem],
+        out_specs=vmem,
+        scratch_shapes=[
+            pltpu.VMEM((members,) + part.shape, part.dtype),
+            dma((members * (rows // chunk),)),
+            dma((members * (rows // chunk),)),
+        ],
+        compiler_params=pltpu.CompilerParams(collective_id=2, has_side_effects=True),
+    )(part)
+
+
 def expert_rows(tok_rows, w_in, w_out):
     partial_sum = jnp.einsum("rd,df->rf", tok_rows, w_in, preferred_element_type=jnp.float32)
-    hidden_total = lax.psum(partial_sum.astype(jnp.bfloat16), "tensor").astype(jnp.float32)
-    hidden = jax.nn.silu(hidden_total).astype(jnp.bfloat16)
+    hidden = hidden_rows(partial_sum.astype(jnp.bfloat16))
     return jnp.einsum("rf,fd->rd", hidden, w_out, preferred_element_type=jnp.float32)
 
 

time: 143 us -> 114 us (0.80)
  waiting for transfers between devices: 17.7 us -> 0 us
  between operations: 13.5 us -> 0.13 us
  Pallas kernels: 64.2 us -> 66.9 us
    psum x1 -> x0, waiting for transfers between devices: 17.7 us -> none  [expert_rows(): lax.psum(partial_sum.astype(jnp.bfloat16), 'tensor').astype(jnp.float32)]
    pallas_call x0 -> x1, Pallas kernels: none -> 4.59 us  [hidden_rows(): pl.pallas_call(functools.partial(hidden_kernel, members, chunk), out_shap...]
    pallas_call x1, Pallas kernels: 28.8 us -> 26.9 us  [send_back(): pl.pallas_call(functools.partial(return_kernel, owners), out_shape=jax.Sh...]
  transfers between devices with their start and end apart: 1 -> 0, of which waited for: 1 -> 0; matrix products, arithmetic and copies ran while one was open for 0% -> 0% of each run, Pallas kernels for 0% -> 0%
where the time goes in v2:
time: 114 us
  Pallas kernels  66.9 us (59%)
  matrix products  37.7 us (33%)
  local copies, waits for them, and re-layouts  3.9 us (3%)
  other arithmetic  2.64 us (2%)
  blocking collectives  2.62 us (2%)
    pallas_call x1, Pallas kernels, dispatch(): pl.pallas_call(functools.partial(dispatch_kernel, owners), out_shape=(jax...  35.4 us
    pallas_call x1, Pallas kernels, send_back(): pl.pallas_call(functools.partial(return_kernel, owners), out_shape=jax.Sh...  26.9 us
    dot_general x1, matrix products, shards(): jnp.einsum('cr,cd->rd', pick_rows, results, preferred_element_type=jnp.fl...  14.1 us
    dot_general x1, matrix products, expert_rows(): jnp.einsum('rd,df->rf', tok_rows, w_in, preferred_element_type=jnp.float32)  11.9 us
    sub x1, matrix products, shards(): powered = jnp.exp(scores - peak_score)  4.64 us
    pallas_call x1, Pallas kernels, hidden_rows(): pl.pallas_call(functools.partial(hidden_kernel, members, chunk), out_shap...  4.59 us
    dot_general x1, matrix products, shards(): jnp.einsum('tgjl,tlgd->tgjd', attention_probs, value_rows, preferred_elem...  3.47 us
    psum x1, blocking collectives, shards(): square_sums = lax.psum(jnp.sum(summed * summed, axis=1), 'tensor')  2.62 us

profile of v2, /device:TPU:0, one launch (start us, length us, event | category | flops | bytes accessed | tf_op | source)
XLA Modules:
  0.0 113.9 jit_solution(15608420688407935868)
XLA Ops:
  0.0 0.8 copy.40
  1.0 0.2 fusion.23
  1.2 0.1 reduce_sum.96
  1.4 0.7 multiply_add_fusion
  2.2 1.2 %reshape.139 = bf16[32,4,6,128]{3,2,1,0:T(8,128)(2,1)S(1)} reshape(bf16[32,3072]{1,0:T(8,128)(2,1)} %param.11) | data formatting | bytes 393216 | tf_op jit(solution)/shard_map/reshape | solution.py:275
  3.4 0.7 iota_compare_fusion.6
  4.1 4.6 %fusion.27 = (f32[32,4,6]{2,1,0:T(4,128)S(1)}, f32[32,4,6,128]{3,2,1,0:T(8,128)S(1)}) fusion(bf16[32,4,6,128]{3,2,1,0:T(8,128)(2,1)S(1)} %reshape.139, pred[32,128]{1,0:T(8,128)(4,1)S(1)} %iota_compare_fusion.6, bf16[32,128,512]{2,1,0:T(8,128)(2,1)} %param.12), kind=kOutput, calls=%fused_computation.51 | convolution fusion | flops 25559168 | bytes 4791296 | tf_op jit(solution)/shard_map/sub | solution.py:284
  8.8 3.5 %fusion.1 = f32[32,4,6,128]{3,2,1,0:T(8,128)S(1)} fusion(f32[32,4,6,128]{3,2,1,0:T(8,128)S(1)} %get-tuple-element.14, f32[32,4,6]{2,1,0:T(4,128)S(1)} %get-tuple-element.13, bf16[32,128,512]{2,1,0:T(8,128)(2,1)} %param.13), kind=kOutput, calls=%fused_computation.2 | convolution fusion | flops 25362432 | bytes 4983808 | tf_op jit(solution)/shard_map/tgjl,tlgd->tgjd/dot_general | solution.py:286
  12.3 0.1 reshape.142
  12.4 0.2 multiply_reduce_fusion
  12.5 2.6 %psum.7 = f32[32]{0:T(128)S(1)} all-reduce(f32[32]{0:T(128)S(1)} %multiply_reduce_fusion), channel_id=1, replica_groups=mesh['dp'=16,'tensor'=2] {'tensor'}, use_global_device_ids=true, to_apply=%region_6.7 | all-reduce | flops 32 | bytes 256 | tf_op jit(solution)/shard_map/psum | solution.py:290
  15.2 1.3 %convolution_convert_fusion.2 = bf16[128,3072]{1,0:T(8,128)(2,1)} fusion(f32[3072]{0:T(1024)S(1)} %convert_element_type.48, f32[32]{0:T(128)S(1)} %add_rsqrt_fusion, f32[32,3072]{1,0:T(8,128)S(1)} %reshape.142, bf16[32,3072]{1,0:T(8,128)(2,1)S(1)} %copy-done, bf16[128,32]{0,1:T(8,128)(2,1)S(1)} %convert_reduce_fusion), kind=kOutput, calls=%fused_computation.9 | convolution fusion | flops 26050560 | bytes 1396864 | tf_op jit(solution)/shard_map/dot_general | solution.py:313
  16.5 0.5 pad.4.counts
  17.0 35.4 %shard_map.100 = (bf16[16,16,3072]{2,1,0:T(8,128)(2,1)}, s32[16,1,128]{2,1,0:T(1,128)}) custom-call(bf16[8,16,3072]{2,1,0:T(8,128)(2,1)} %bitcast.44, s32[1,128]{1,0:T(1,128)} %pad.4.counts), custom_call_target="tpu_custom_call" | custom-call | tf_op jit(solution)/shard_map/pallas_call | solution.py:112
  52.4 0.8 copy.42
  53.2 0.1 fusion.26
  53.3 0.1 select_reduce_fusion.3
  53.6 11.9 %convolution_convert_fusion.part = bf16[96,4096]{1,0:T(8,128)(2,1)} fusion(bf16[3072,4096]{1,0:T(8,128)(2,1)} %param.18, bf16[256,3072]{1,0:T(8,128)(2,1)} %bitcast.43, s32[256]{0:T(256)S(1)} %select_n.38), kind=kOutput, calls=%fused_computation.1 | convolution fusion | flops 2567626752 | bytes 27526144 | tf_op jit(solution)/shard_map/rd,df->rf/dot_general | solution.py:263
  65.5 4.6 %shard_map.101 = bf16[96,4096]{1,0:T(8,128)(2,1)} custom-call(bf16[96,4096]{1,0:T(8,128)(2,1)} %convolution_convert_fusion.part), custom_call_target="tpu_custom_call" | custom-call | tf_op jit(solution)/shard_map/pallas_call | solution.py:248
  70.2 14.1 %convolution_convert_fusion.1 = bf16[256,3072]{1,0:T(8,128)(2,1)} fusion(bf16[96,4096]{1,0:T(8,128)(2,1)} %shard_map.101, bf16[4096,3072]{1,0:T(8,128)(2,1)} %param.19, s32[256]{0:T(256)S(1)} %select_n.38), kind=kOutput, calls=%fused_computation.8 | convolution fusion | flops 2568019968 | bytes 27526144 | tf_op jit(solution)/shard_map/cr,cd->rd/dot_general | solution.py:341
  84.2 26.9 %shard_map.102 = bf16[8,16,3072]{2,1,0:T(8,128)(2,1)} custom-call(bf16[16,16,3072]{2,1,0:T(8,128)(2,1)} %bitcast.42), custom_call_target="tpu_custom_call" | custom-call | tf_op jit(solution)/shard_map/pallas_call | solution.py:182
  111.2 0.2 select_reduce_fusion.1
  111.3 0.1 reduce_sum.102
  111.6 2.2 %fusion.7 = bf16[32,3072]{1,0:T(8,128)(2,1)} fusion(f32[128,32]{0,1:T(8,128)S(1)} %select_reduce_fusion, bf16[128,3072]{1,0:T(8,128)(2,1)} %bitcast.45, f32[32,3072]{1,0:T(8,128)S(1)} %reshape.142, bf16[32,3072]{1,0:T(8,128)(2,1)S(1)} %copy-done), kind=kOutput, calls=%fused_computation.13 | convolution fusion | flops 151388160 | bytes 1589248 | tf_op jit(solution)/shard_map/st,sd->td/dot_general | solution.py:354
  (20 shorter events, 0.8 us)
Async XLA Ops:
  8.8 3.6 %copy-start = (bf16[32,3072]{1,0:T(8,128)(2,1)S(1)}, bf16[32,3072]{1,0:T(8,128)(2,1)}, u32[]{:S(2)}) copy-start(bf16[32,3072]{1,0:T(8,128)(2,1)} %param.10) | copy-start | bytes 589828
  8.8 6.4 %copy-start.1 = (bf16[3072]{0:T(1024)(128)(2,1)S(1)}, bf16[3072]{0:T(1024)(128)(2,1)}, u32[]{:S(2)}) copy-start(bf16[3072]{0:T(1024)(128)(2,1)} %param.15) | copy-start | bytes 18436
  70.1 41.4 %copy-start.2 = (f32[32,2]{0,1:T(2,128)S(1)}, f32[32,2]{0,1:T(2,128)}, u32[]{:S(2)}) copy-start(f32[32,2]{0,1:T(2,128)} %param.17) | copy-start | bytes 772
